TPU v7x, 32 devices: a whole 2x2x4 slice. The times are simulated.
32 devices in a mesh: seq: 16 (over z, x, core), chan: 2 (over y).
Axes of the slice: x: 2, y: 2, z: 4, core: 2. Of those that a mesh axis runs over, the one named last changes fastest.
Arguments:
- signal: bfloat16 [524288, 256], P('seq', 'chan'), parts along dimension 1, may hold values from -6 to 6
- gate_values: bfloat16 [524288, 256], P('seq', 'chan'), parts along dimension 1, may hold values from -4 to 4
- skip_gain: float32 [256], P('chan'), parts along dimension 0, may hold values from 0.25 to 2
- filter_spectrum: bfloat16 [2, 512, 1024, 256], P(None, 'seq', None, 'chan'), parts along dimension 3, may hold values from -4 to 4, as said below
Outputs:
- gated_output: bfloat16 [524288, 256], P('seq', 'chan'), parts along dimension 1
There are 2 independent parts, one for each index of `chan`. A program takes and returns all parts, laid end to end along the dimension named above; each array names one. Nothing has to cross between parts.
Inputs may be any that keep to these rules, and one draw needn't show every extreme that they name: `filter_spectrum`: the spectrum of a real filter: the complex entry at frequency k equals the conjugate of the entry at frequency (524288 - k) mod 524288.
All inputs are finite; a program needn't handle non-finite values.
Results may differ from a plain program's by a relative error of at most 0.0085.
Values may be sent and summed in bfloat16 or wider, within the bound.
No kernel may reach another device: no remote copies, remote signals or barrier semaphores. Data moves between devices by JAX's collectives and lax.ppermute only.
A program may use at most 256 MiB of HBM per device.

v0:
```python
import math

import jax
import jax.numpy as jnp
from jax import lax
from jax.sharding import PartitionSpec as P

OUTER = 1024
INNER = 512
SEQ = 524288


def tables(length):
    indices = lax.iota(jnp.int32, length)
    angles = (
        2.0 * math.pi / length * (indices[:, None] * indices[None, :] % length).astype(jnp.float32)
    )
    return (jnp.cos(angles).astype(jnp.bfloat16), jnp.sin(angles).astype(jnp.bfloat16))


def twiddle(c_values, b_values, length):
    angles = (
        2.0
        * math.pi
        / length
        * (c_values[:, None] * b_values[None, :] % length).astype(jnp.float32)
    )
    return (jnp.cos(angles), jnp.sin(angles))


def spectral_product(spectrum, filter_cols):
    spec_re = spectrum[0].astype(jnp.float32)
    spec_im = spectrum[1].astype(jnp.float32)
    filter_re = filter_cols[0].astype(jnp.float32)
    filter_im = filter_cols[1].astype(jnp.float32)
    return jnp.stack(
        [spec_re * filter_re - spec_im * filter_im, spec_re * filter_im + spec_im * filter_re]
    ).astype(jnp.bfloat16)


def local(signal, gate_values, skip_gain, filter_spectrum):
    shards = lax.axis_size("seq")
    own_index = lax.axis_index("seq")
    channels = signal.shape[1]
    outer_loc = OUTER // shards
    inner_loc = INNER // shards
    cos_a, sin_a = tables(OUTER)
    cos_b, sin_b = tables(INNER)
    inner_table = jnp.stack([cos_b, sin_b])
    outer_scale = 1.0 / math.sqrt(OUTER)
    inner_scale = 1.0 / math.sqrt(INNER)
    own_b = own_index * inner_loc + lax.iota(jnp.int32, inner_loc)
    own_c = own_index * outer_loc + lax.iota(jnp.int32, outer_loc)
    cols_cos, cols_sin = twiddle(lax.iota(jnp.int32, OUTER), own_b, SEQ)
    rows_cos, rows_sin = twiddle(own_c, lax.iota(jnp.int32, INNER), SEQ)
    cols_cos = cols_cos[:, :, None]
    cols_sin = cols_sin[:, :, None]
    rows_cos = rows_cos[:, :, None]
    rows_sin = rows_sin[:, :, None]
    signal_grid = signal.reshape(outer_loc, INNER, channels)
    pieces = lax.all_to_all(signal_grid, "seq", split_axis=1, concat_axis=0, tiled=True)
    breadth = pieces.shape[2]
    flattened = pieces.reshape(OUTER, inner_loc * breadth)
    fwd_re = jnp.dot(cos_a, flattened, preferred_element_type=jnp.float32).reshape(
        OUTER, inner_loc, breadth
    )
    fwd_im = -jnp.dot(sin_a, flattened, preferred_element_type=jnp.float32).reshape(
        OUTER, inner_loc, breadth
    )
    columns = jnp.stack(
        [
            (fwd_re * cols_cos + fwd_im * cols_sin) * outer_scale,
            (fwd_im * cols_cos - fwd_re * cols_sin) * outer_scale,
        ]
    ).astype(jnp.bfloat16)
    partials = jnp.einsum(
        "tdb,scbk->tscdk",
        inner_table,
        lax.all_to_all(columns, "seq", split_axis=1, concat_axis=2, tiled=True),
        preferred_element_type=jnp.float32,
    )
    spectrum = jnp.stack(
        [
            (partials[0, 0] + partials[1, 1]) * inner_scale,
            (partials[0, 1] - partials[1, 0]) * inner_scale,
        ]
    ).astype(jnp.bfloat16)
    filter_cols = lax.all_to_all(filter_spectrum, "seq", split_axis=2, concat_axis=1, tiled=True)
    product = spectral_product(spectrum, jnp.swapaxes(filter_cols, 1, 2))
    partials = jnp.einsum(
        "tbd,scdk->tscbk", inner_table, product, preferred_element_type=jnp.float32
    )
    back_re = (partials[0, 0] - partials[1, 1]) * inner_scale
    back_im = (partials[0, 1] + partials[1, 0]) * inner_scale
    rotated = jnp.stack(
        [back_re * rows_cos - back_im * rows_sin, back_re * rows_sin + back_im * rows_cos]
    ).astype(jnp.bfloat16)
    pieces = lax.all_to_all(rotated, "seq", split_axis=2, concat_axis=1, tiled=True)
    breadth = pieces.shape[3]
    convolved = (
        jnp.dot(
            cos_a, pieces[0].reshape(OUTER, inner_loc * breadth), preferred_element_type=jnp.float32
        )
        - jnp.dot(
            sin_a, pieces[1].reshape(OUTER, inner_loc * breadth), preferred_element_type=jnp.float32
        )
    ) * outer_scale
    by_columns = convolved.reshape(OUTER, inner_loc, breadth).astype(jnp.bfloat16)
    convolved = lax.all_to_all(by_columns, "seq", split_axis=0, concat_axis=1, tiled=True).reshape(
        outer_loc * INNER, channels
    )
    result = gate_values.astype(jnp.float32) * (
        convolved.astype(jnp.float32) + skip_gain[None, :] * signal.astype(jnp.float32)
    )
    return result.astype(jnp.bfloat16)


def solution(mesh):
    return jax.shard_map(
        local,
        mesh=mesh,
        in_specs=(P("seq", "chan"), P("seq", "chan"), P("chan"), P(None, "seq", None, "chan")),
        out_specs=P("seq", "chan"),
        check_vma=False,
    )
```

profile of v0, /device:TPU:1, one launch (start us, length us, event | category | flops | bytes accessed | tf_op | source)
XLA Modules:
  0.0 1843.1 jit_solution(5718546721229991774)
XLA Ops:
  0.0 12.2 copy.61
  19.5 18.6 %copy.71 = bf16[2,32,1024,128]{3,1,0,2:T(8,128)(2,1)} copy(bf16[2,32,1024,128]{3,2,1,0:T(8,128)(2,1)} %param.7) | data formatting | bytes 33554432 | tf_op args[3]
  38.1 132.6 %all-to-all-done = bf16[64,512,128]{2,0,1:T(8,128)(2,1)} async-done(((bf16[64,512,128]{2,0,1:T(8,128)(2,1)}), bf16[64,512,128]{2,0,1:T(8,128)(2,1)}, u32[]{:S(2)}, u32[]{:S(2)}) %all-to-all-start) | async-done | bytes 8388640 | tf_op jit(solution)/shard_map/all_to_all | solution.py:61
  170.7 35.9 %all-to-all-start.2 = ((bf16[2,32,1024,128]{3,1,0,2:T(8,128)(2,1)}), bf16[2,32,1024,128]{3,1,0,2:T(8,128)(2,1)}, u32[]{:S(2)}, u32[]{:S(2)}) async-start(bf16[2,32,1024,128]{3,1,0,2:T(8,128)(2,1)} %copy.71), calls=%async_computation.2 | async-start | bytes 33554432 | tf_op jit(solution)/shard_map/all_to_all | solution.py:88
  207.2 15.7 fusion.88
  222.9 13.8 copy.63
  236.7 15.3 copy.108
  252.0 11.9 copy.64
  264.0 30.3 %fusion.35 = f32[1024,32,128]{2,0,1:T(8,128)} fusion(bf16[32,128,1024]{2,1,0:T(8,128)(2,1)} %bitcast.161), kind=kOutput, calls=%fused_computation.60 | convolution fusion | flops 8605663232 | bytes 25165824 | tf_op jit(solution)/shard_map/dot_general | solution.py:67
  294.3 19.2 %fusion.16 = (bf16[1,1024,32,128]{3,1,2,0:T(8,128)(2,1)S(1)}, bf16[1,1024,32,128]{3,1,2,0:T(8,128)(2,1)}) fusion(f32[1024,32,128]{2,0,1:T(8,128)} %fusion.35, f32[1024,32]{0,1:T(8,128)S(1)} %get-tuple-element.15, f32[1024,32]{0,1:T(8,128)S(1)} %get-tuple-element.14, bf16[32,128,1024]{2,1,0:T(8,128)(2,1)S(1)} %bitcast.162, bf16[1024,1024,1]{1,0,2:T(8,128)(2,1)S(1)} %fusion.88), kind=kOutput, calls=%fused_computation.37 | convolution fusion | flops 8636071936 | bytes 44302336 | tf_op jit(solution)/shard_map/dot_general | solution.py:64
  319.7 40.3 %copy.65 = bf16[2,1024,32,128]{3,2,0,1:T(8,128)(2,1)} copy(bf16[2,1024,32,128]{3,1,2,0:T(8,128)(2,1)S(1)} %pad_maximum_fusion) | data formatting | bytes 33554432 | tf_op jit(solution)/shard_map/stack | solution.py:70
  360.0 143.8 %all-to-all-done.2 = bf16[2,32,1024,128]{3,1,0,2:T(8,128)(2,1)} async-done(((bf16[2,32,1024,128]{3,1,0,2:T(8,128)(2,1)}), bf16[2,32,1024,128]{3,1,0,2:T(8,128)(2,1)}, u32[]{:S(2)}, u32[]{:S(2)}) %all-to-all-start.2) | async-done | bytes 16777248 | tf_op jit(solution)/shard_map/all_to_all | solution.py:88
  503.8 70.0 %all-to-all-start.1 = ((bf16[2,1024,32,128]{3,2,0,1:T(8,128)(2,1)}), bf16[2,1024,32,128]{3,2,0,1:T(8,128)(2,1)}, u32[]{:S(2)}, u32[]{:S(2)}) async-start(bf16[2,1024,32,128]{3,2,0,1:T(8,128)(2,1)} %copy.65), calls=%async_computation.1 | async-start | bytes 33554432 | tf_op jit(solution)/shard_map/all_to_all | solution.py:79
  578.8 17.8 copy.73
  596.6 23.9 %copy.74 = bf16[2,512,64,128]{1,3,2,0:T(8,128)(2,1)} copy(bf16[2,512,64,128]{3,2,1,0:T(8,128)(2,1)} %bitcast.154) | data formatting | bytes 33554432 | tf_op jit(solution)/shard_map/all_to_all | solution.py:88
  620.5 250.4 %all-to-all-done.1 = bf16[2,1024,32,128]{3,2,0,1:T(8,128)(2,1)} async-done(((bf16[2,1024,32,128]{3,2,0,1:T(8,128)(2,1)}), bf16[2,1024,32,128]{3,2,0,1:T(8,128)(2,1)}, u32[]{:S(2)}, u32[]{:S(2)}) %all-to-all-start.1) | async-done | bytes 16777248 | tf_op jit(solution)/shard_map/all_to_all | solution.py:79
  870.9 15.3 copy.67
  886.2 31.7 %convolution_bitcast_fusion.1 = f32[2,2,64,512,128]{3,4,0,2,1:T(8,128)} fusion(bf16[2,64,512,128,1]{3,2,4,1,0:T(8,128)(2,1)} %bitcast.160, bf16[1,512,512]{2,1,0:T(8,128)(2,1)S(1)} %get-tuple-element.18, bf16[1,512,512]{2,1,0:T(8,128)(2,1)S(1)} %get-tuple-element.19), kind=kOutput, calls=%fused_computation.1 | convolution fusion | flops 17181966336 | bytes 84934656 | tf_op jit(solution)/shard_map/tdb,scbk->tscdk/dot_general | solution.py:76
  917.9 36.8 %fusion.1 = (bf16[1,64,512,128]{2,3,1,0:T(8,128)(2,1)}, bf16[1,64,512,128]{2,3,1,0:T(8,128)(2,1)}, bf16[1,64,512,128]{2,3,1,0:T(8,128)(2,1)}) fusion(bf16[2,64,512,128]{2,3,1,0:T(8,128)(2,1)} %bitcast.151, f32[2,2,64,512,128]{3,4,0,2,1:T(8,128)} %convolution_bitcast_fusion.1), kind=kLoop, calls=%fused_computation.7 | loop fusion | flops 58720256 | bytes 109051904 | tf_op jit(solution)/shard_map/convert.5
  954.8 15.5 fusion.3
  970.3 31.5 %convolution_bitcast_fusion = f32[2,2,64,512,128]{3,4,0,2,1:T(8,128)} fusion(bf16[1,64,512,128]{2,3,1,0:T(8,128)(2,1)} %fusion.3, bf16[1,64,512,128]{2,3,1,0:T(8,128)(2,1)} %get-tuple-element.5, bf16[1,512,512]{2,1,0:T(8,128)(2,1)S(1)} %get-tuple-element.18, bf16[1,512,512]{2,1,0:T(8,128)(2,1)S(1)} %get-tuple-element.19), kind=kOutput, calls=%fused_computation | convolution fusion | flops 17215520768 | bytes 84934656 | tf_op jit(solution)/shard_map/tbd,scdk->tscbk/dot_general | solution.py:90
  1001.8 26.6 %subtract_convert_fusion = (bf16[1,64,512,128]{2,3,1,0:T(8,128)(2,1)S(1)}, bf16[1,64,512,128]{2,3,1,0:T(8,128)(2,1)}) fusion(f32[64,512]{1,0:T(8,128)S(1)} %get-tuple-element.17, f32[64,512]{1,0:T(8,128)S(1)} %get-tuple-element.16, f32[2,2,64,512,128]{3,4,0,2,1:T(8,128)} %convolution_bitcast_fusion), kind=kLoop, calls=%fused_computation.34 | loop fusion | flops 41943040 | bytes 84148224 | tf_op jit(solution)/shard_map/convert.3
  1028.5 10.5 pad_maximum_fusion.1
  1038.9 22.7 %copy.78 = bf16[2,64,512,128]{3,1,0,2:T(8,128)(2,1)} copy(bf16[2,64,512,128]{2,3,1,0:T(8,128)(2,1)} %pad_maximum_fusion.1) | data formatting | bytes 33554432 | tf_op jit(solution)/shard_map/stack | solution.py:95
  1061.7 431.9 %all_to_all.75 = bf16[2,64,512,128]{3,1,0,2:T(8,128)(2,1)S(1)} all-to-all(bf16[2,64,512,128]{3,1,0,2:T(8,128)(2,1)} %copy.78), channel_id=1, replica_groups=mesh['seq'=16,'chan'=2] {'seq'}, dimensions={2} | all-to-all | bytes 33554432 | tf_op jit(solution)/shard_map/all_to_all | solution.py:98
  1493.6 36.1 %copy.79 = bf16[2,64,512,128]{3,2,1,0:T(8,128)(2,1)S(1)} copy(bf16[2,64,512,128]{3,1,0,2:T(8,128)(2,1)S(1)} %all_to_all.75) | data formatting | bytes 33554432 | tf_op jit(solution)/shard_map/all_to_all | solution.py:98
  1545.3 30.8 %fusion.26 = f32[1024,4096]{1,0:T(8,128)} fusion(bf16[128,8,32,128]{3,2,1,0:T(8,128)(2,1)} %bitcast.164), kind=kOutput, calls=%fused_computation.45 | convolution fusion | flops 8605663232 | bytes 25165824 | tf_op jit(solution)/shard_map/dot_general | solution.py:101
  1585.0 32.8 %fusion.18 = bf16[128,8,32,128]{3,1,2,0:T(8,128)(2,1)} fusion(f32[1024,4096]{1,0:T(8,128)} %fusion.26, bf16[128,8,32,128]{3,2,1,0:T(8,128)(2,1)} %bitcast.163), kind=kOutput, calls=%fused_computation.39 | convolution fusion | flops 8618246144 | bytes 33554432 | tf_op jit(solution)/shard_map/dot_general | solution.py:104
  1617.8 9.4 copy.98
  1627.2 188.6 %all_to_all.76 = bf16[1024,32,128]{2,1,0:T(8,128)(2,1)} all-to-all(bf16[1024,32,128]{2,1,0:T(8,128)(2,1)} %bitcast.158), channel_id=1, replica_groups=mesh['seq'=16,'chan'=2] {'seq'}, dimensions={0} | all-to-all | bytes 16777216 | tf_op jit(solution)/shard_map/all_to_all | solution.py:109
  1815.8 11.6 copy.82
  1827.4 15.2 fusion.15
  (14 shorter events, 43.4 us)
Async XLA Ops:
  12.2 158.5 %all-to-all-start = ((bf16[64,512,128]{2,0,1:T(8,128)(2,1)}), bf16[64,512,128]{2,0,1:T(8,128)(2,1)}, u32[]{:S(2)}, u32[]{:S(2)}) async-start(bf16[64,512,128]{2,0,1:T(8,128)(2,1)} %copy.61), calls=%async_computation | async-start | bytes 16777216 | tf_op jit(solution)/shard_map/all_to_all | solution.py:61
  170.7 333.2 %all-to-all-start.2 = ((bf16[2,32,1024,128]{3,1,0,2:T(8,128)(2,1)}), bf16[2,32,1024,128]{3,1,0,2:T(8,128)(2,1)}, u32[]{:S(2)}, u32[]{:S(2)}) async-start(bf16[2,32,1024,128]{3,1,0,2:T(8,128)(2,1)} %copy.71), calls=%async_computation.2 | async-start | bytes 33554432 | tf_op jit(solution)/shard_map/all_to_all | solution.py:88
  263.9 30.3 %copy-start = (bf16[4096,1024]{1,0:T(8,128)(2,1)S(1)}, bf16[4096,1024]{1,0:T(8,128)(2,1)}, u32[]{:S(2)}) copy-start(bf16[4096,1024]{1,0:T(8,128)(2,1)} %copy.64) | copy-start | bytes 25165828
  503.8 367.1 %all-to-all-start.1 = ((bf16[2,1024,32,128]{3,2,0,1:T(8,128)(2,1)}), bf16[2,1024,32,128]{3,2,0,1:T(8,128)(2,1)}, u32[]{:S(2)}, u32[]{:S(2)}) async-start(bf16[2,1024,32,128]{3,2,0,1:T(8,128)(2,1)} %copy.65), calls=%async_computation.1 | async-start | bytes 33554432 | tf_op jit(solution)/shard_map/all_to_all | solution.py:79
  1815.8 11.6 copy-start.1
where the time goes:
time: 1850 us; the launch traced here: 1840 us
  blocking collectives  621 us (34%)
  waiting for transfers between devices  527 us (28%)
  local copies, waits for them, and re-layouts  273 us (15%)
  matrix products  176 us (10%)
  other arithmetic  132 us (7%)
  starting transfers between devices  113 us (6%)
    all_to_all x1, blocking collectives, local(): lax.all_to_all(rotated, 'seq', split_axis=2, concat_axis=1, tiled=True)  432 us
    all_to_all x1, waiting for transfers between devices, local(): lax.all_to_all(columns, 'seq', split_axis=1, concat_axis=2, tiled=True)  250 us
    all_to_all x1, blocking collectives, local(): lax.all_to_all(by_columns, 'seq', split_axis=0, concat_axis=1, tiled=True)  189 us
    all_to_all x1, waiting for transfers between devices, local(): lax.all_to_all(filter_spectrum, 'seq', split_axis=2, concat_axis=1, tiled...  144 us
    all_to_all x1, waiting for transfers between devices, local(): lax.all_to_all(signal_grid, 'seq', split_axis=1, concat_axis=0, tiled=True)  133 us
    another operation x3, other arithmetic  79 us
    all_to_all x1, starting transfers between devices, local(): lax.all_to_all(columns, 'seq', split_axis=1, concat_axis=2, tiled=True)  70 us
    unnamed x7, local copies, waits for them, and re-layouts  43.3 us
  transfers between devices with their start and end apart: 3, of which 3 were waited for; matrix products, arithmetic and copies ran while one was open for 12% of the time, Pallas kernels for 0%

commit v1 on v0

v1 whole, which is shorter than its diff:
```python
import functools
import math

import jax
import jax.numpy as jnp
from jax import lax
from jax.experimental import pallas as pl
from jax.experimental.pallas import tpu as pltpu
from jax.sharding import PartitionSpec as P


CHUNKS = 2
LANES = 128
NT = (((1,), (1,)), ((), ()))
TN = (((0,), (0,)), ((), ()))
VMEM = 60 * 1024 * 1024


def angles(rows, cols, length):
    return 2.0 * math.pi / length * (rows[:, None] * cols[None, :] % length).astype(jnp.float32)


def make_tables(outer, inner, half, d_rows, zero):
    i_out = lax.iota(jnp.int32, outer) + zero
    i_in = lax.iota(jnp.int32, inner) + zero
    ang = angles(i_out, i_out, outer)
    ta = jnp.concatenate([jnp.cos(ang), jnp.sin(ang)], axis=1).astype(jnp.bfloat16)
    ang = angles(d_rows, i_in, inner)
    cb, sb = jnp.cos(ang).astype(jnp.bfloat16), jnp.sin(ang).astype(jnp.bfloat16)
    g = jnp.concatenate(
        [jnp.concatenate([cb, sb], axis=1), jnp.concatenate([-sb, cb], axis=1)], axis=0
    )
    gi = g.T
    length = outer * inner
    ang = angles(i_out, i_in, length)
    scale = 1.0 / math.sqrt(outer)
    wc, ws = jnp.cos(ang) * scale, jnp.sin(ang) * scale
    ang = angles(i_in, i_out, length)
    scale = 2.0 / math.sqrt(inner)
    vc, vs = jnp.cos(ang) * scale, jnp.sin(ang) * scale
    alt = jnp.where((half == 0) & (i_in % 2 == 1), -1.0, 1.0).astype(jnp.float32)
    row_sign = jnp.broadcast_to(alt[None, :], (8, inner))
    col_sign = jnp.broadcast_to(alt[:, None], (inner, LANES))
    return ta, g, gi, wc, ws, vc, vs, row_sign, col_sign


def conv_kernel(spot_ref, x_ref, *refs, n_h, block):
    h_refs = refs[:n_h]
    ta_ref, g_ref, gi_ref, wc_ref, ws_ref, vc_ref, vs_ref, rs_ref, cs_ref = refs[n_h : n_h + 9]
    o_ref, f_ref, xs_ref, r_ref = refs[n_h + 9 :]
    outer, inner = wc_ref.shape
    half = inner // 2
    f32, b16 = jnp.float32, jnp.bfloat16
    n_src, rows_src, _ = x_ref.shape
    n_ch = pl.num_programs(0)
    ch = pl.program_id(0)
    cc = n_src * rows_src // outer
    tiles = inner // LANES
    inner_scale = 1.0 / math.sqrt(inner)

    @pl.when(ch == 0)
    def _():
        def spread(s, carry):
            v = x_ref[s].astype(f32)
            for t in range(tiles):
                f_ref[t, pl.ds(pl.multiple_of(s * rows_src, rows_src), rows_src), :] = v[
                    :, t * LANES : (t + 1) * LANES
                ]
            return carry

        lax.fori_loop(0, n_src, spread, 0)

    def pick(j, carry):
        for t in range(tiles):
            v = f_ref[t, pl.ds(ch + j * (block * cc), block, stride=cc), :]
            xs_ref[pl.ds(pl.multiple_of(j * block, block), block), t * LANES : (t + 1) * LANES] = (
                v.astype(b16)
            )
        return carry

    lax.fori_loop(0, outer // block, pick, 0)

    def step(i, carry):
        at = pl.multiple_of(i * block, block)
        rows = pl.ds(at, block)
        x = xs_ref[...]
        f_c = jnp.dot(ta_ref[rows, :outer], x, preferred_element_type=f32)
        f_s = jnp.dot(ta_ref[rows, outer:], x, preferred_element_type=f32)
        wc, ws = wc_ref[rows, :], ws_ref[rows, :]
        q_re = (f_c * wc - f_s * ws).astype(b16)
        q_im = (-(f_s * wc + f_c * ws)).astype(b16)
        q = jnp.concatenate([q_re, q_im], axis=1)
        s = lax.dot_general(g_ref[...], q, NT, preferred_element_type=f32) * inner_scale
        s_re = s[:half].astype(b16).astype(f32)
        s_im = s[half:].astype(b16).astype(f32)
        first = (
            (lax.broadcasted_iota(jnp.int32, (half, block), 0) == spot_ref[0])
            & (lax.broadcasted_iota(jnp.int32, (half, block), 1) == 0)
            & (i == 0)
        )
        h_re = jnp.concatenate([h[0, 0, :, rows] for h in h_refs], axis=0).astype(f32)
        h_im = jnp.concatenate([h[0, 1, :, rows] for h in h_refs], axis=0).astype(f32)
        other = jnp.sum(jnp.where(first, h_im, 0.0)[:, :LANES])
        h_re = jnp.where(first, 0.5 * h_re, h_re)
        h_im = jnp.where(first, 0.0, h_im)
        p = jnp.concatenate(
            [(s_re * h_re - s_im * h_im).astype(b16), (s_re * h_im + s_im * h_re).astype(b16)],
            axis=0,
        )
        u = jnp.dot(gi_ref[...], p, preferred_element_type=f32)
        lone = jnp.sum(q_re[:8, :].astype(f32)[:1, :] * rs_ref[:1, :], axis=1, keepdims=True)
        lone = (lone * inner_scale).astype(b16).astype(f32)
        lone = (lone * other).astype(b16).astype(f32) * 0.5
        fix = jnp.where(
            lax.broadcasted_iota(jnp.int32, (inner, LANES), 1) == 0, cs_ref[...] * lone, 0.0
        )
        fix = jnp.concatenate([fix, jnp.zeros((inner, block - LANES), f32)], axis=1)
        u_re = u[:inner] + fix
        u_im = u[inner:]
        vc, vs = vc_ref[:, rows], vs_ref[:, rows]
        r_ref[:, rows] = (u_re * vc - u_im * vs).astype(b16)
        r_ref[:, pl.ds(pl.multiple_of(outer + at, block), block)] = (
            -(u_re * vs + u_im * vc)
        ).astype(b16)
        return carry

    lax.fori_loop(0, outer // block, step, 0)
    outer_scale = 1.0 / math.sqrt(outer)

    def last(j, carry):
        at = pl.multiple_of(j * block, block)
        y = lax.dot_general(
            ta_ref[pl.ds(at, block), :], r_ref[...], NT, preferred_element_type=f32
        )
        y = y * outer_scale
        for t in range(tiles):
            f_ref[t, pl.ds(ch + j * (block * cc), block, stride=cc), :] = y[
                :, t * LANES : (t + 1) * LANES
            ]
        return carry

    lax.fori_loop(0, outer // block, last, 0)

    @pl.when(ch == n_ch - 1)
    def _():
        def collect(s, carry):
            for t in range(tiles):
                v = f_ref[t, pl.ds(pl.multiple_of(s * rows_src, rows_src), rows_src), :]
                o_ref[s, :, t * LANES : (t + 1) * LANES] = v.astype(b16)
            return carry

        lax.fori_loop(0, n_src, collect, 0)


def convolve(spot, x, hs, tables, block=256):
    n_src, rows_src, inner = x.shape
    outer = tables[0].shape[0]
    cc = n_src * rows_src // outer
    const = lambda t: pl.BlockSpec(t.shape, lambda i: (0,) * t.ndim, pipeline_mode=pl.Buffered(1))
    flops = 2 * cc * outer * outer * inner * 6
    return pl.pallas_call(
        functools.partial(conv_kernel, n_h=len(hs), block=block),
        grid=(cc,),
        in_specs=[
            pl.BlockSpec(memory_space=pltpu.SMEM),
            const(x),
            *[pl.BlockSpec((1,) + h.shape[1:], lambda i: (i, 0, 0, 0)) for h in hs],
            *[const(t) for t in tables],
        ],
        out_specs=const(x),
        out_shape=jax.ShapeDtypeStruct(x.shape, jnp.bfloat16),
        scratch_shapes=[
            pltpu.VMEM((inner // LANES, outer * cc, LANES), jnp.float32),
            pltpu.VMEM((outer, inner), jnp.bfloat16),
            pltpu.VMEM((inner, 2 * outer), jnp.bfloat16),
        ],
        compiler_params=pltpu.CompilerParams(vmem_limit_bytes=VMEM),
        cost_estimate=pl.CostEstimate(
            flops=flops, bytes_accessed=2 * (2 * x.size + 8 * hs[0].size), transcendentals=0
        ),
        name="convolve",
    )(spot, x, *hs, *tables)


def order(shards, ch_dev, chunks, ap):
    cc = ch_dev // chunks
    r = lax.iota(jnp.int32, chunks * shards * ap * cc)
    c = r % cc
    a = r // cc % ap
    dest = r // (cc * ap) % shards
    k = r // (cc * ap * shards)
    return a * (shards * ch_dev) + dest * ch_dev + k * cc + c


def split_kernel(sel_ref, x_ref, *o_refs, ap):
    a_blk, inner, _ = x_ref.shape
    rows = sel_ref.shape[0] // len(o_refs)

    def step(g, carry):
        x = jnp.concatenate([x_ref[g * ap + j] for j in range(ap)], axis=1)
        y = lax.dot_general(sel_ref[...], x, NT, preferred_element_type=jnp.float32)
        y = y.astype(jnp.bfloat16)
        for k, o_ref in enumerate(o_refs):
            n_dest = o_ref.shape[0]
            per = rows // n_dest
            o_ref[:, pl.ds(pl.multiple_of(g * per, per), per), :] = y[
                k * rows : (k + 1) * rows
            ].reshape(n_dest, per, inner)
        return carry

    lax.fori_loop(0, a_blk // ap, step, 0)


def split_signal(signal, shards, chunks):
    a_loc, inner, channels = signal.shape
    ch_dev = channels // shards
    cc = ch_dev // chunks
    ap = max(1, 8 // cc)
    a_blk = min(a_loc, max(8, 16 // cc, ap))
    cols = order(shards, ch_dev, chunks, ap)
    sel = (cols[:, None] == lax.iota(jnp.int32, ap * channels)[None, :]).astype(jnp.bfloat16)
    out = jax.ShapeDtypeStruct((shards, a_loc * cc, inner), jnp.bfloat16)
    return pl.pallas_call(
        functools.partial(split_kernel, ap=ap),
        grid=(a_loc // a_blk,),
        in_specs=[
            pl.BlockSpec(sel.shape, lambda i: (0, 0)),
            pl.BlockSpec((a_blk, inner, channels), lambda i: (i, 0, 0)),
        ],
        out_specs=[pl.BlockSpec((shards, a_blk * cc, inner), lambda i: (0, i, 0))] * chunks,
        out_shape=[out] * chunks,
        compiler_params=pltpu.CompilerParams(vmem_limit_bytes=VMEM),
        cost_estimate=pl.CostEstimate(
            flops=2 * signal.size * sel.shape[0], bytes_accessed=4 * signal.size, transcendentals=0
        ),
        name="split_signal",
    )(sel, signal)


def merge_kernel(sel_ref, skip_ref, sig_ref, gate_ref, *refs, ap):
    y_refs, o_ref = refs[:-1], refs[-1]
    a_blk, inner, channels = sig_ref.shape
    f32 = jnp.float32

    def step(g, carry):
        parts = []
        for y_ref in y_refs:
            n_src, rows_blk, _ = y_ref.shape
            per = rows_blk * ap // a_blk
            y = y_ref[:, pl.ds(pl.multiple_of(g * per, per), per), :]
            parts.append(y.reshape(n_src * per, inner))
        y = jnp.concatenate(parts, axis=0)
        z = lax.dot_general(y, sel_ref[...], TN, preferred_element_type=f32)
        for j in range(ap):
            at = g * ap + j
            conv = z[:, j * channels : (j + 1) * channels]
            total = conv + skip_ref[...] * sig_ref[at].astype(f32)
            o_ref[at] = (gate_ref[at].astype(f32) * total).astype(o_ref.dtype)
        return carry

    lax.fori_loop(0, a_blk // ap, step, 0)


def merge(ys, signal, gate, skip, shards):
    a_loc, inner, channels = signal.shape
    chunks = len(ys)
    ch_dev = channels // shards
    cc = ch_dev // chunks
    ap = max(1, 8 // cc)
    a_blk = min(a_loc, max(8, 16 // cc, ap))
    cols = order(shards, ch_dev, chunks, ap)
    sel = (cols[:, None] == lax.iota(jnp.int32, ap * channels)[None, :]).astype(jnp.bfloat16)
    whole = pl.BlockSpec((a_blk, inner, channels), lambda i: (i, 0, 0))
    return pl.pallas_call(
        functools.partial(merge_kernel, ap=ap),
        grid=(a_loc // a_blk,),
        in_specs=[
            pl.BlockSpec(sel.shape, lambda i: (0, 0)),
            pl.BlockSpec((1, channels), lambda i: (0, 0)),
            whole,
            whole,
            *[pl.BlockSpec((shards, a_blk * cc, inner), lambda i: (0, i, 0))] * chunks,
        ],
        out_specs=whole,
        out_shape=jax.ShapeDtypeStruct(signal.shape, jnp.bfloat16),
        compiler_params=pltpu.CompilerParams(vmem_limit_bytes=VMEM),
        cost_estimate=pl.CostEstimate(
            flops=2 * signal.size * sel.shape[0], bytes_accessed=8 * signal.size, transcendentals=0
        ),
        name="merge",
    )(sel, skip, signal, gate, *ys)


def exchange(v):
    return lax.all_to_all(v, "seq", split_axis=0, concat_axis=0, tiled=True)


def layer(signal, gate_values, skip_gain, filter_spectrum):
    shards = lax.axis_size("seq")
    me = lax.axis_index("seq")
    positions, channels = signal.shape
    _, d_loc, outer, _ = filter_spectrum.shape
    inner = d_loc * shards
    a_loc = positions // inner
    ch_dev = channels // shards
    chunks = CHUNKS
    cc = ch_dev // chunks
    group = shards // 2
    half = me // group
    mine = me % group
    zero = me // shards
    barrier = lax.optimization_barrier

    row = lax.ppermute(filter_spectrum[0, 0, 0, :], "seq", [(0, group), (group, 0)])

    signal = signal.reshape(a_loc, inner, channels)
    xs = list(split_signal(signal, shards, chunks))
    xs[0], row = barrier((xs[0], row))
    got = [None] * chunks
    got[0] = exchange(xs[0])

    filt = filter_spectrum.transpose(3, 0, 1, 2)
    spot_im = jnp.where(mine == 0, row, filt[:, 1, 0, 0])
    filt = filt.at[:, 1, 0, 0].set(spot_im)
    filt = filt.reshape(2, group, chunks, cc, 2, d_loc, outer)
    cut = [
        [filt[half, (mine + s) % group, k] for s in range(group)] for k in range(chunks)
    ]
    hs = []
    for k in range(chunks):
        pieces = []
        for s, piece in enumerate(cut[k]):
            if s:
                pairs = [
                    (b * group + i, b * group + (i + s) % group)
                    for b in range(2)
                    for i in range(group)
                ]
                piece = lax.ppermute(piece, "seq", pairs)
            pieces.append(piece)
        hs.append(pieces)

    shift = lax.iota(jnp.int32, group)
    src = (mine - shift) % group
    d_rows = (half * group + src)[:, None] * d_loc + lax.iota(jnp.int32, d_loc)[None, :]
    tables = make_tables(outer, inner, half, d_rows.reshape(-1), zero)
    spot = (mine * d_loc).reshape(1)

    for k in range(1, chunks):
        extra = (tables, cut) if k == 1 else ()
        xs[k], got[k - 1], extra = barrier((xs[k], got[k - 1], extra))
        if k == 1:
            tables = extra[0]
        got[k] = exchange(xs[k])
    ys = []
    for k in range(chunks):
        out = convolve(spot, got[k], hs[k], tables)
        if k + 1 < chunks:
            out, hs[k + 1] = barrier((out, hs[k + 1]))
        ys.append(exchange(out))
    out = merge(ys, signal, gate_values.reshape(signal.shape), skip_gain[None, :], shards)
    return out.reshape(positions, channels)


def solution(mesh):
    return jax.shard_map(
        layer,
        mesh=mesh,
        in_specs=(P("seq", "chan"), P("seq", "chan"), P("chan"), P(None, "seq", None, "chan")),
        out_specs=P("seq", "chan"),
        check_vma=False,
    )
```

time: 1850 us -> 540 us (0.29)
  blocking collectives: 621 us -> 112 us
  waiting for transfers between devices: 527 us -> 90.6 us
  local copies, waits for them, and re-layouts: 273 us -> 40.5 us
  matrix products: 176 us -> 0 us
  Pallas kernels: 0 us -> 145 us
  other arithmetic: 132 us -> 46.2 us
    all_to_all x2 -> x1, blocking collectives: 621 us -> 112 us  [exchange(): return lax.all_to_all(v, 'seq', split_axis=0, concat_axis=0, tiled=True)]
    all_to_all x3, waiting for transfers between devices: 527 us -> 20.3 us  [exchange(): return lax.all_to_all(v, 'seq', split_axis=0, concat_axis=0, tiled=True)]
    dot_general x6 -> x0, matrix products: 176 us -> none  [the longest x1 32.8 us: local(): jnp.dot(sin_a, pieces[1].reshape(OUTER, inner_loc * breadth), preferred_e...]
    pallas_call x0 -> x4, Pallas kernels: none -> 145 us  [the longest x2 116 us: convolve(): pl.pallas_call(functools.partial(conv_kernel, n_h=len(hs), block=block),...]
    all_to_all x5 -> x0, local copies, waits for them, and re-layouts: 107 us -> none  [the longest x2 41.7 us: local(): lax.all_to_all(filter_spectrum, 'seq', split_axis=2, concat_axis=1, tiled...]
    all_to_all x3, starting transfers between devices: 113 us -> 32.1 us  [exchange(): return lax.all_to_all(v, 'seq', split_axis=0, concat_axis=0, tiled=True)]
    another operation x5 -> x2, other arithmetic: 95.7 us -> 17.3 us
    ppermute x0 -> x15, starting transfers between devices: none -> 72.2 us  [the longest x14 71.6 us: layer(): piece = lax.ppermute(piece, 'seq', pairs)]
  transfers between devices with their start and end apart: 3 -> 18, of which waited for: 3 -> 7; matrix products, arithmetic and copies ran while one was open for 12% -> 15% of each run, Pallas kernels for 0% -> 24%
where the time goes in v1:
time: 540 us; the launch traced here: 538 us
  Pallas kernels  145 us (27%)
  blocking collectives  112 us (21%)
  starting transfers between devices  104 us (19%)
  waiting for transfers between devices  90.6 us (17%)
  other arithmetic  46.2 us (9%)
  local copies, waits for them, and re-layouts  40.5 us (8%)
    pallas_call x2, Pallas kernels, convolve(): pl.pallas_call(functools.partial(conv_kernel, n_h=len(hs), block=block),...  116 us
    all_to_all x1, blocking collectives, exchange(): return lax.all_to_all(v, 'seq', split_axis=0, concat_axis=0, tiled=True)  112 us
    ppermute x14, starting transfers between devices, layer(): piece = lax.ppermute(piece, 'seq', pairs)  71.6 us
    ppermute x14, waiting for transfers between devices, layer(): piece = lax.ppermute(piece, 'seq', pairs)  70.3 us
    all_to_all x3, starting transfers between devices, exchange(): return lax.all_to_all(v, 'seq', split_axis=0, concat_axis=0, tiled=True)  32.1 us
    unnamed x7, local copies, waits for them, and re-layouts  24.7 us
    all_to_all x3, waiting for transfers between devices, exchange(): return lax.all_to_all(v, 'seq', split_axis=0, concat_axis=0, tiled=True)  20.3 us
    another operation x2, other arithmetic  17.3 us
  transfers between devices with their start and end apart: 18, of which 7 were waited for; matrix products, arithmetic and copies ran while one was open for 15% of the time, Pallas kernels for 24%

profile of v1, /device:TPU:1, one launch (start us, length us, event | category | flops | bytes accessed | tf_op | source)
XLA Modules:
  0.0 538.3 jit_solution(176208550211111263)
XLA Ops:
  2.1 12.6 %split_signal.1 = (bf16[16,256,512]{2,1,0:T(8,128)(2,1)}, bf16[16,256,512]{2,1,0:T(8,128)(2,1)}) custom-call(bf16[256,256]{1,0:T(8,128)(2,1)} %fusion.12.sel_ref, bf16[64,512,128]{2,1,0:T(8,128)(2,1)} %bitcast.48), custom_call_target="tpu_custom_call" | custom-call | flops 2147483648 | bytes 16777216 | tf_op jit(solution)/shard_map/split_signal/pallas_call | solution.py:223
  14.8 9.6 %all-to-all-start = ((bf16[16,256,512]{2,1,0:T(8,128)(2,1)}), bf16[16,256,512]{2,1,0:T(8,128)(2,1)}, u32[]{:S(2)}, u32[]{:S(2)}) async-start(bf16[16,256,512]{2,1,0:T(8,128)(2,1)} %get-tuple-element.43), calls=%async_computation | async-start | bytes 8388608 | tf_op jit(solution)/shard_map/all_to_all | solution.py:295
  24.4 23.5 %copy.27 = bf16[2,32,1024,128]{2,1,0,3:T(8,128)(2,1)} copy(bf16[2,32,1024,128]{3,2,1,0:T(8,128)(2,1)} %param.9) | data formatting | bytes 33554432 | tf_op args[3]
  48.1 2.0 slice_reduce_fusion
  50.0 2.2 fusion.13
  52.2 2.5 sine_convert_fusion.1
  55.9 17.3 %cosine_convert_fusion = (bf16[1024,1024]{1,0:T(8,128)(2,1)S(1)}, bf16[1024,1024]{1,0:T(8,128)(2,1)S(1)}) fusion(s32[1024]{0:T(1024)S(1)} %iota_add_fusion.1), kind=kLoop, calls=%fused_computation.10 | loop fusion | flops 16777216 | bytes 4198400 | tf_op jit(solution)/shard_map/convert
  73.2 2.5 pad_maximum_fusion.refs_8_
  75.7 9.8 %sine_multiply_fusion = (f32[512,1024]{1,0:T(8,128)}, f32[512,1024]{1,0:T(8,128)}) fusion(s32[1024]{0:T(1024)S(1)} %iota_add_fusion.1, s32[512]{0:T(512)S(1)} %iota_add_fusion.2), kind=kLoop, calls=%fused_computation.27 | loop fusion | flops 8388608 | bytes 4200448 | tf_op jit(solution)/shard_map/mul | solution.py:40
  85.5 9.9 %sine_multiply_fusion.1 = (f32[1024,512]{1,0:T(8,128)}, f32[1024,512]{1,0:T(8,128)}) fusion(s32[512]{0:T(512)S(1)} %iota_add_fusion.2, s32[1024]{0:T(1024)S(1)} %iota_add_fusion.1), kind=kLoop, calls=%fused_computation.29 | loop fusion | flops 8388608 | bytes 4200448 | tf_op jit(solution)/shard_map/mul | solution.py:37
  95.5 3.7 scatter.4
  99.2 6.4 %dynamic-slice_bitcast_fusion = (bf16[4,2,32,1024]{3,2,1,0:T(8,128)(2,1)S(1)}, bf16[4,2,32,1024]{3,2,1,0:T(8,128)(2,1)S(1)}, bf16[4,2,32,1024]{3,2,1,0:T(8,128)(...) fusion(bf16[2,8,2,4,2,32,1024]{6,5,4,3,2,1,0:T(8,128)(2,1)} %bi, ...), kind=kLoop, calls=%fused_computation.40 | loop fusion | bytes 16777252 | tf_op jit(solution)/shard_map/squeeze | solution.py:327
  107.1 16.0 %all-to-all-start.2 = ((bf16[16,256,512]{2,1,0:T(8,128)(2,1)}), bf16[16,256,512]{2,1,0:T(8,128)(2,1)}, u32[]{:S(2)}, u32[]{:S(2)}) async-start(bf16[16,256,512]{2,1,0:T(8,128)(2,1)} %get-tuple-element.56), calls=%async_computation.2 | async-start | bytes 8388608 | tf_op jit(solution)/shard_map/all_to_all | solution.py:295
  123.1 1.6 collective-permute-start.1
  126.6 2.3 collective-permute-start.5
  128.8 34.2 %collective-permute-done.1.refs_1_ = bf16[4,2,32,1024]{3,2,1,0:T(8,128)(2,1)} collective-permute-done((bf16[4,2,32,1024]{3,2,1,0:T(8,128)(2,1)}, bf16[4,2,32,1024]{3,2,1,0:T(8,128)(2,1)}, u32[]{:S(2)}, u32[]{:S(2)}) %collective-permute-start.1) | collective-permute-done | bytes 524320 | tf_op jit(solution)/shard_map/ppermute | solution.py:339
  163.0 24.5 %collective-permute-start.6 = (bf16[4,2,32,1024]{3,2,1,0:T(8,128)(2,1)}, bf16[4,2,32,1024]{3,2,1,0:T(8,128)(2,1)}, u32[]{:S(2)}, u32[]{:S(2)}) collective-permute-start(bf16[4,2,32,1024]{3,2,1,0:T(8,128)(2,1)} %get-tuple-element.74), channel_id=1, source_target_pairs={{0,12},{2,14},{4,0},{6,2},{8,4},{10,6},{12,8},{14,10},{16,28},{18,... | collective-permute-start | bytes 1572872 | tf_op jit(solution)/shard_map/ppermute | solution.py:339
  187.5 28.7 %collective-permute-done.2.refs_2_ = bf16[4,2,32,1024]{3,2,1,0:T(8,128)(2,1)} collective-permute-done((bf16[4,2,32,1024]{3,2,1,0:T(8,128)(2,1)}, bf16[4,2,32,1024]{3,2,1,0:T(8,128)(2,1)}, u32[]{:S(2)}, u32[]{:S(2)}) %collective-permute-start.2) | collective-permute-done | bytes 524320 | tf_op jit(solution)/shard_map/ppermute | solution.py:339
  217.2 5.6 %collective-permute-start.10 = (bf16[4,2,32,1024]{3,2,1,0:T(8,128)(2,1)}, bf16[4,2,32,1024]{3,2,1,0:T(8,128)(2,1)}, u32[]{:S(2)}, u32[]{:S(2)}) collective-permute-start(bf16[4,2,32,1024]{3,2,1,0:T(8,128)(2,1)} %get-tuple-element.69), channel_id=1, source_target_pairs={{0,6},{2,8},{4,10},{6,12},{8,14},{10,0},{12,2},{14,4},{16,22},{18,... | collective-permute-start | bytes 1572872 | tf_op jit(solution)/shard_map/ppermute | solution.py:339
  226.1 13.5 %collective-permute-start.12 = (bf16[4,2,32,1024]{3,2,1,0:T(8,128)(2,1)}, bf16[4,2,32,1024]{3,2,1,0:T(8,128)(2,1)S(1)}, u32[]{:S(2)}, u32[]{:S(2)}) collective-permute-start(bf16[4,2,32,1024]{3,2,1,0:T(8,128)(2,1)} %get-tuple-element.67), channel_id=1, source_target_pairs={{0,10},{2,12},{4,14},{6,0},{8,2},{10,4},{12,6},{14,8},{16,26},{18,... | collective-permute-start | bytes 1572872 | tf_op jit(solution)/shard_map/ppermute | solution.py:339
  239.5 7.4 %collective-permute-start.13 = (bf16[4,2,32,1024]{3,2,1,0:T(8,128)(2,1)S(1)}, bf16[4,2,32,1024]{3,2,1,0:T(8,128)(2,1)S(1)}, u32[]{:S(2)}, u32[]{:S(2)}) collective-permute-start(bf16[4,2,32,1024]{3,2,1,0:T(8,128)(2,1)S(1)} %get-tuple-element.66), channel_id=1, source_target_pairs={{0,12},{2,14},{4,0},{6,2},{8,4},{10,6},{12,8},{14,10},{16,28},{18,... | collective-permute-start | bytes 1572872 | tf_op jit(solution)/shard_map/ppermute | solution.py:339
  246.9 2.0 collective-permute-start.14
  248.9 2.0 collective-permute-done.10.refs_3_
  250.9 5.6 %collective-permute-start.8 = (bf16[4,2,32,1024]{3,2,1,0:T(8,128)(2,1)S(1)}, bf16[4,2,32,1024]{3,2,1,0:T(8,128)(2,1)}, u32[]{:S(2)}, u32[]{:S(2)}) collective-permute-start(bf16[4,2,32,1024]{3,2,1,0:T(8,128)(2,1)S(1)} %get-tuple-element.71), channel_id=1, source_target_pairs={{0,2},{2,4},{4,6},{6,8},{8,10},{10,12},{12,14},{14,0},{16,18},{18,... | collective-permute-start | bytes 1572872 | tf_op jit(solution)/shard_map/ppermute | solution.py:339
  256.5 3.8 collective-permute-done.11.refs_4_
  260.3 6.0 %collective-permute-start.9 = (bf16[4,2,32,1024]{3,2,1,0:T(8,128)(2,1)S(1)}, bf16[4,2,32,1024]{3,2,1,0:T(8,128)(2,1)}, u32[]{:S(2)}, u32[]{:S(2)}) collective-permute-start(bf16[4,2,32,1024]{3,2,1,0:T(8,128)(2,1)S(1)} %get-tuple-element.70), channel_id=1, source_target_pairs={{0,4},{2,6},{4,8},{6,10},{8,12},{10,14},{12,0},{14,2},{16,20},{18,... | collective-permute-start | bytes 1572872 | tf_op jit(solution)/shard_map/ppermute | solution.py:339
  266.3 57.9 %convolve.2 = bf16[16,256,512]{2,1,0:T(8,128)(2,1)} custom-call(s32[1]{0:T(128)} %bitcast.3.spot_ref, bf16[16,256,512]{2,1,0:T(8,128)(2,1)} %all-to-all-done.x_ref, bf16[4,2,32,1024]{3,2,1,0:T(8,128)(2,1)} %get-tuple-element.80.refs_0_, bf16[4,2,32,1024]{3,2,1,0:T(8,128)(2,1)} %collective-permute-done.1.refs_1_, ...), custom_call_target="tpu_custom_call" | custom-call | flops 25769803776 | bytes 12582912 | tf_op jit(solution)/shard_map/convolve/pallas_call | solution.py:161
  325.5 6.5 %all-to-all-start.1 = ((bf16[16,256,512]{2,1,0:T(8,128)(2,1)}), bf16[16,256,512]{2,1,0:T(8,128)(2,1)}, u32[]{:S(2)}, u32[]{:S(2)}) async-start(bf16[16,256,512]{2,1,0:T(8,128)(2,1)} %convolve.2), calls=%async_computation.1 | async-start | bytes 8388608 | tf_op jit(solution)/shard_map/all_to_all | solution.py:295
  332.0 57.9 %convolve.3 = bf16[16,256,512]{2,1,0:T(8,128)(2,1)} custom-call(s32[1]{0:T(128)} %bitcast.3.spot_ref, bf16[16,256,512]{2,1,0:T(8,128)(2,1)} %all-to-all-done.2.x_ref, bf16[4,2,32,1024]{3,2,1,0:T(8,128)(2,1)} %get-tuple-element.57.refs_0_, bf16[4,2,32,1024]{3,2,1,0:T(8,128)(2,1)} %collective-permute-done.8.refs_1_, ...), custom_call_target="tpu_custom_call" | custom-call | flops 25769803776 | bytes 12582912 | tf_op jit(solution)/shard_map/convolve/pallas_call | solution.py:161
  389.9 20.3 %all-to-all-done.1.refs_0_ = bf16[16,256,512]{2,1,0:T(8,128)(2,1)} async-done(((bf16[16,256,512]{2,1,0:T(8,128)(2,1)}), bf16[16,256,512]{2,1,0:T(8,128)(2,1)}, u32[]{:S(2)}, u32[]{:S(2)}) %all-to-all-start.1) | async-done | bytes 4194336 | tf_op jit(solution)/shard_map/all_to_all | solution.py:295
  410.1 111.8 %all_to_all.20.refs_1_ = bf16[16,256,512]{2,1,0:T(8,128)(2,1)} all-to-all(bf16[16,256,512]{2,1,0:T(8,128)(2,1)} %convolve.3), channel_id=1, replica_groups=mesh['seq'=16,'chan'=2] {'seq'}, dimensions={0} | all-to-all | bytes 8388608 | tf_op jit(solution)/shard_map/all_to_all | solution.py:295
  522.0 16.3 %merge.1 = bf16[64,512,128]{2,1,0:T(8,128)(2,1)} custom-call(bf16[256,256]{1,0:T(8,128)(2,1)} %fusion.12.sel_ref, f32[1,128]{1,0:T(1,128)} %bitcast.51, bf16[64,512,128]{2,1,0:T(8,128)(2,1)} %bitcast.49, bf16[64,512,128]{2,1,0:T(8,128)(2,1)} %bitcast.50, bf16[16,256,512]{2,1,0:T(8,128)(2,1)} %all-to-all-done.1.refs_0_, bf16[16,256,512]{2,1,0:T(8,128)(2,1)} %all_to_all.20.refs_1_), custom_call_target="tpu_custom_call" | custom-call | flops 2147483648 | bytes 33554432 | tf_op jit(solution)/shard_map/merge/pallas_call | solution.py:274
  (40 shorter events, 12.4 us)
Async XLA Ops:
  0.7 14.1 %collective-permute-start = (bf16[128]{0:T(256)(128)(2,1)S(1)}, bf16[128]{0:T(256)(128)(2,1)S(1)}, u32[]{:S(2)}, u32[]{:S(2)}) collective-permute-start(bf16[128]{0:T(256)(128)(2,1)S(1)} %slice_bitcast_fusion), channel_id=1, source_target_pairs={{0,16},{16,0},{1,17},{17,1}} | collective-permute-start | bytes 776 | tf_op jit(solution)/shard_map/ppermute | solution.py:314
  14.8 90.9 %all-to-all-start = ((bf16[16,256,512]{2,1,0:T(8,128)(2,1)}), bf16[16,256,512]{2,1,0:T(8,128)(2,1)}, u32[]{:S(2)}, u32[]{:S(2)}) async-start(bf16[16,256,512]{2,1,0:T(8,128)(2,1)} %get-tuple-element.43), calls=%async_computation | async-start | bytes 8388608 | tf_op jit(solution)/shard_map/all_to_all | solution.py:295
  107.1 218.2 %all-to-all-start.2 = ((bf16[16,256,512]{2,1,0:T(8,128)(2,1)}), bf16[16,256,512]{2,1,0:T(8,128)(2,1)}, u32[]{:S(2)}, u32[]{:S(2)}) async-start(bf16[16,256,512]{2,1,0:T(8,128)(2,1)} %get-tuple-element.56), calls=%async_computation.2 | async-start | bytes 8388608 | tf_op jit(solution)/shard_map/all_to_all | solution.py:295
  123.1 39.9 %collective-permute-start.1 = (bf16[4,2,32,1024]{3,2,1,0:T(8,128)(2,1)}, bf16[4,2,32,1024]{3,2,1,0:T(8,128)(2,1)}, u32[]{:S(2)}, u32[]{:S(2)}) collective-permute-start(bf16[4,2,32,1024]{3,2,1,0:T(8,128)(2,1)} %get-tuple-element.79), channel_id=1, source_target_pairs={{0,2},{2,4},{4,6},{6,8},{8,10},{10,12},{12,14},{14,0},{16,18},{18,... | collective-permute-start | bytes 1572872 | tf_op jit(solution)/shard_map/ppermute | solution.py:339
  124.7 91.4 %collective-permute-start.2 = (bf16[4,2,32,1024]{3,2,1,0:T(8,128)(2,1)}, bf16[4,2,32,1024]{3,2,1,0:T(8,128)(2,1)}, u32[]{:S(2)}, u32[]{:S(2)}) collective-permute-start(bf16[4,2,32,1024]{3,2,1,0:T(8,128)(2,1)} %get-tuple-element.78), channel_id=1, source_target_pairs={{0,4},{2,6},{4,8},{6,10},{8,12},{10,14},{12,0},{14,2},{16,20},{18,... | collective-permute-start | bytes 1572872 | tf_op jit(solution)/shard_map/ppermute | solution.py:339
  125.9 91.3 %collective-permute-start.3 = (bf16[4,2,32,1024]{3,2,1,0:T(8,128)(2,1)}, bf16[4,2,32,1024]{3,2,1,0:T(8,128)(2,1)}, u32[]{:S(2)}, u32[]{:S(2)}) collective-permute-start(bf16[4,2,32,1024]{3,2,1,0:T(8,128)(2,1)} %get-tuple-element.77), channel_id=1, source_target_pairs={{0,6},{2,8},{4,10},{6,12},{8,14},{10,0},{12,2},{14,4},{16,22},{18,... | collective-permute-start | bytes 1572872 | tf_op jit(solution)/shard_map/ppermute | solution.py:339
  126.3 96.5 %collective-permute-start.4 = (bf16[4,2,32,1024]{3,2,1,0:T(8,128)(2,1)}, bf16[4,2,32,1024]{3,2,1,0:T(8,128)(2,1)}, u32[]{:S(2)}, u32[]{:S(2)}) collective-permute-start(bf16[4,2,32,1024]{3,2,1,0:T(8,128)(2,1)} %get-tuple-element.76), channel_id=1, source_target_pairs={{0,8},{2,10},{4,12},{6,14},{8,0},{10,2},{12,4},{14,6},{16,24},{18,... | collective-permute-start | bytes 1572872 | tf_op jit(solution)/shard_map/ppermute | solution.py:339
  126.6 99.5 %collective-permute-start.5 = (bf16[4,2,32,1024]{3,2,1,0:T(8,128)(2,1)}, bf16[4,2,32,1024]{3,2,1,0:T(8,128)(2,1)}, u32[]{:S(2)}, u32[]{:S(2)}) collective-permute-start(bf16[4,2,32,1024]{3,2,1,0:T(8,128)(2,1)} %get-tuple-element.75), channel_id=1, source_target_pairs={{0,10},{2,12},{4,14},{6,0},{8,2},{10,4},{12,6},{14,8},{16,26},{18,... | collective-permute-start | bytes 1572872 | tf_op jit(solution)/shard_map/ppermute | solution.py:339
  163.0 76.6 %collective-permute-start.6 = (bf16[4,2,32,1024]{3,2,1,0:T(8,128)(2,1)}, bf16[4,2,32,1024]{3,2,1,0:T(8,128)(2,1)}, u32[]{:S(2)}, u32[]{:S(2)}) collective-permute-start(bf16[4,2,32,1024]{3,2,1,0:T(8,128)(2,1)} %get-tuple-element.74), channel_id=1, source_target_pairs={{0,12},{2,14},{4,0},{6,2},{8,4},{10,6},{12,8},{14,10},{16,28},{18,... | collective-permute-start | bytes 1572872 | tf_op jit(solution)/shard_map/ppermute | solution.py:339
  216.1 30.8 %collective-permute-start.7 = (bf16[4,2,32,1024]{3,2,1,0:T(8,128)(2,1)}, bf16[4,2,32,1024]{3,2,1,0:T(8,128)(2,1)}, u32[]{:S(2)}, u32[]{:S(2)}) collective-permute-start(bf16[4,2,32,1024]{3,2,1,0:T(8,128)(2,1)} %get-tuple-element.73), channel_id=1, source_target_pairs={{0,14},{2,0},{4,2},{6,4},{8,6},{10,8},{12,10},{14,12},{16,30},{18,... | collective-permute-start | bytes 1572872 | tf_op jit(solution)/shard_map/ppermute | solution.py:339
  217.2 33.7 %collective-permute-start.10 = (bf16[4,2,32,1024]{3,2,1,0:T(8,128)(2,1)}, bf16[4,2,32,1024]{3,2,1,0:T(8,128)(2,1)}, u32[]{:S(2)}, u32[]{:S(2)}) collective-permute-start(bf16[4,2,32,1024]{3,2,1,0:T(8,128)(2,1)} %get-tuple-element.69), channel_id=1, source_target_pairs={{0,6},{2,8},{4,10},{6,12},{8,14},{10,0},{12,2},{14,4},{16,22},{18,... | collective-permute-start | bytes 1572872 | tf_op jit(solution)/shard_map/ppermute | solution.py:339
  222.8 37.4 %collective-permute-start.11 = (bf16[4,2,32,1024]{3,2,1,0:T(8,128)(2,1)}, bf16[4,2,32,1024]{3,2,1,0:T(8,128)(2,1)}, u32[]{:S(2)}, u32[]{:S(2)}) collective-permute-start(bf16[4,2,32,1024]{3,2,1,0:T(8,128)(2,1)} %get-tuple-element.68), channel_id=1, source_target_pairs={{0,8},{2,10},{4,12},{6,14},{8,0},{10,2},{12,4},{14,6},{16,24},{18,... | collective-permute-start | bytes 1572872 | tf_op jit(solution)/shard_map/ppermute | solution.py:339
  226.1 98.1 %collective-permute-start.12 = (bf16[4,2,32,1024]{3,2,1,0:T(8,128)(2,1)}, bf16[4,2,32,1024]{3,2,1,0:T(8,128)(2,1)S(1)}, u32[]{:S(2)}, u32[]{:S(2)}) collective-permute-start(bf16[4,2,32,1024]{3,2,1,0:T(8,128)(2,1)} %get-tuple-element.67), channel_id=1, source_target_pairs={{0,10},{2,12},{4,14},{6,0},{8,2},{10,4},{12,6},{14,8},{16,26},{18,... | collective-permute-start | bytes 1572872 | tf_op jit(solution)/shard_map/ppermute | solution.py:339
  239.5 84.7 %collective-permute-start.13 = (bf16[4,2,32,1024]{3,2,1,0:T(8,128)(2,1)S(1)}, bf16[4,2,32,1024]{3,2,1,0:T(8,128)(2,1)S(1)}, u32[]{:S(2)}, u32[]{:S(2)}) collective-permute-start(bf16[4,2,32,1024]{3,2,1,0:T(8,128)(2,1)S(1)} %get-tuple-element.66), channel_id=1, source_target_pairs={{0,12},{2,14},{4,0},{6,2},{8,4},{10,6},{12,8},{14,10},{16,28},{18,... | collective-permute-start | bytes 1572872 | tf_op jit(solution)/shard_map/ppermute | solution.py:339
  246.9 77.3 %collective-permute-start.14 = (bf16[4,2,32,1024]{3,2,1,0:T(8,128)(2,1)S(1)}, bf16[4,2,32,1024]{3,2,1,0:T(8,128)(2,1)S(1)}, u32[]{:S(2)}, u32[]{:S(2)}) collective-permute-start(bf16[4,2,32,1024]{3,2,1,0:T(8,128)(2,1)S(1)} %get-tuple-element.65), channel_id=1, source_target_pairs={{0,14},{2,0},{4,2},{6,4},{8,6},{10,8},{12,10},{14,12},{16,30},{18,... | collective-permute-start | bytes 1572872 | tf_op jit(solution)/shard_map/ppermute | solution.py:339
  250.9 73.3 %collective-permute-start.8 = (bf16[4,2,32,1024]{3,2,1,0:T(8,128)(2,1)S(1)}, bf16[4,2,32,1024]{3,2,1,0:T(8,128)(2,1)}, u32[]{:S(2)}, u32[]{:S(2)}) collective-permute-start(bf16[4,2,32,1024]{3,2,1,0:T(8,128)(2,1)S(1)} %get-tuple-element.71), channel_id=1, source_target_pairs={{0,2},{2,4},{4,6},{6,8},{8,10},{10,12},{12,14},{14,0},{16,18},{18,... | collective-permute-start | bytes 1572872 | tf_op jit(solution)/shard_map/ppermute | solution.py:339
  260.3 65.0 %collective-permute-start.9 = (bf16[4,2,32,1024]{3,2,1,0:T(8,128)(2,1)S(1)}, bf16[4,2,32,1024]{3,2,1,0:T(8,128)(2,1)}, u32[]{:S(2)}, u32[]{:S(2)}) collective-permute-start(bf16[4,2,32,1024]{3,2,1,0:T(8,128)(2,1)S(1)} %get-tuple-element.70), channel_id=1, source_target_pairs={{0,4},{2,6},{4,8},{6,10},{8,12},{10,14},{12,0},{14,2},{16,20},{18,... | collective-permute-start | bytes 1572872 | tf_op jit(solution)/shard_map/ppermute | solution.py:339
  324.2 1.1 copy-start
  324.2 1.2 copy-start.1
  324.3 1.0 copy-start.2
  325.5 84.7 %all-to-all-start.1 = ((bf16[16,256,512]{2,1,0:T(8,128)(2,1)}), bf16[16,256,512]{2,1,0:T(8,128)(2,1)}, u32[]{:S(2)}, u32[]{:S(2)}) async-start(bf16[16,256,512]{2,1,0:T(8,128)(2,1)} %convolve.2), calls=%async_computation.1 | async-start | bytes 8388608 | tf_op jit(solution)/shard_map/all_to_all | solution.py:295
